TPU v7x, 32 devices: a whole 2x2x4 slice. The times are simulated.
32 devices in a mesh: groups: 2 (over x), blk: 8 (over z, y), span: 2 (over core).
Axes of the slice: x: 2, y: 2, z: 4, core: 2. Of those that a mesh axis runs over, the one named last changes fastest.
Arguments:
- embeddings: bfloat16 [8192, 768], P(('groups', 'blk', 'span')), parts along dimension 0, may hold values from -6 to 6
- owner_ids: int32 [8192, 1], P(('groups', 'blk', 'span')), parts along dimension 0, may hold values from 0 to 7, as said below
- local_ids: int32 [8192], P(('groups', 'blk', 'span')), parts along dimension 0, may hold values from 0 to 15, as said below
- cluster_map: int32 [256], P('groups'), parts along dimension 0, may hold values from 0 to 127, as said below
Outputs:
- nearest: float32 [8192], P(('groups', 'blk', 'span')), parts along dimension 0
- centroid_cosine: float32 [8192], P(('groups', 'blk', 'span')), parts along dimension 0
There are 2 independent parts, one for each index of `groups`. A program takes and returns all parts, laid end to end along the dimension named above; each array names one. Nothing has to cross between parts.
Inputs may be any that keep to these rules, and one draw needn't show every extreme that they name: `owner_ids`: at most 64 rows of one device name the same owner; in every draw one owner is named by exactly 64 rows of every device. `local_ids`: of the rows of one device that name one owner, at most 16 have local id 0; in every draw one owner receives exactly 16 rows with local id 0 from every device. In every draw some clusters with a local id other than 0 have exactly one row in the whole shard. cluster_map[o * 16 + l] = o * 16 + l for l > 0. For l = 0 the owners fall into runs of 1 to 3 consecutive owners, and every owner of a run has the value of the run's first owner; some run has 3 owners.
All inputs are finite; a program needn't handle non-finite values.
Results may differ from a plain program's by a relative error of at most 0.0017.
Values may be sent and summed in bfloat16 or wider, within the bound.
No kernel may reach another device: no remote copies, remote signals or barrier semaphores. Data moves between devices by JAX's collectives and lax.ppermute only.
A program may use at most 64 MiB of HBM per device.

v0:
```python
import jax
import jax.numpy as jnp
from jax import lax
from jax.sharding import PartitionSpec as P

GIANT_SPAN = 3


def passed_along(value, axis, steps):
    count = lax.axis_size(axis)
    first, last = (max(0, -steps), min(count, count - steps))
    return lax.ppermute(value, axis, [(source, source + steps) for source in range(first, last)])


def normalize(values):
    wide = values.astype(jnp.float32)
    scale = lax.rsqrt(jnp.sum(wide * wide, axis=1, keepdims=True) + 1e-06)
    return (wide * scale).astype(jnp.bfloat16)


def masked_scores(left, left_tags, right, right_tags):
    scores = lax.dot_general(
        left, right, (((1,), (1,)), ((), ())), preferred_element_type=jnp.float32
    )
    same = (left_tags[:, None] == right_tags[None, :]) & (left_tags[:, None] > 0)
    return jnp.where(same, scores, -1.0)


def body(embeddings, owner_ids, local_ids, cluster_map):
    rows = embeddings.shape[0]
    width = embeddings.shape[1]
    owners = lax.axis_size("blk")
    capacity = 2 * rows // owners
    slots = owners * capacity
    clusters = cluster_map.shape[0]
    owned = clusters // owners
    unit = normalize(embeddings)
    destination = owner_ids[:, 0]
    flat = destination * owned + local_ids
    table = jnp.arange(clusters, dtype=jnp.int32)
    cluster = jnp.sum(jnp.where(flat[:, None] == table[None, :], cluster_map[None, :], 0), axis=1)
    onehot = (destination[:, None] == jnp.arange(owners, dtype=jnp.int32)[None, :]).astype(
        jnp.int32
    )
    before = jnp.cumsum(onehot, axis=0) - onehot
    rank = jnp.sum(before * onehot, axis=1)
    position = destination * capacity + rank
    send_rows = jnp.zeros((slots, width), jnp.bfloat16).at[position].set(unit)
    send_tags = jnp.zeros((slots,), jnp.int32).at[position].set(cluster + 1)
    arrived, arrived_tags = (
        lax.all_to_all(
            send_rows.reshape(owners, capacity, width),
            "blk",
            split_axis=0,
            concat_axis=0,
            tiled=True,
        ),
        lax.all_to_all(
            send_tags.reshape(owners, capacity), "blk", split_axis=0, concat_axis=0, tiled=True
        ),
    )
    mine = arrived.reshape(slots, width)
    my_tags = arrived_tags.reshape(slots)
    chip, chip_tags = (
        lax.all_gather(mine, "span", axis=0, tiled=True),
        lax.all_gather(my_tags, "span", axis=0, tiled=True),
    )
    half = lax.axis_index("span")
    block_index = lax.axis_index("blk")
    own_tags = lax.dynamic_slice_in_dim(cluster_map, block_index * owned, owned, 0) + 1
    local = masked_scores(mine, my_tags, chip, chip_tags)
    itself = (
        jnp.arange(2 * slots, dtype=jnp.int32)[None, :]
        == (jnp.arange(slots, dtype=jnp.int32) + half * slots)[:, None]
    )
    best = jnp.max(jnp.where(itself, -1.0, local), axis=1)
    share_limit = 2 * owners * max(1, capacity // 4)
    shared_mask = chip_tags == own_tags[0]
    packed_rank = jnp.cumsum(shared_mask.astype(jnp.int32)) - 1
    target = jnp.where(shared_mask, packed_rank, share_limit)
    packed = jnp.zeros((share_limit, width), jnp.bfloat16).at[target].set(chip, mode="drop")
    packed_tags = jnp.zeros((share_limit,), jnp.int32).at[target].set(chip_tags, mode="drop")
    upper = (packed, packed_tags)
    lower = (packed, packed_tags)
    for step in range(1, GIANT_SPAN):
        upper = passed_along((upper[0], upper[1]), "blk", 1)
        lower = passed_along((lower[0], lower[1]), "blk", -1)
        for other in (upper, lower):
            best = jnp.maximum(
                best, jnp.max(masked_scores(mine, my_tags, other[0], other[1]), axis=1)
            )
    chosen = cluster[:, None] == table[None, :]
    partial_sums = lax.dot_general(
        chosen.astype(jnp.bfloat16),
        unit,
        (((0,), (0,)), ((), ())),
        preferred_element_type=jnp.float32,
    )
    sums = lax.psum(partial_sums, ("blk", "span"))
    length = jnp.sqrt(jnp.sum(sums * sums, axis=1, keepdims=True))
    direction = sums / jnp.maximum(length, 1.0)
    centroid_cosine = jnp.sum(unit.astype(jnp.float32) * direction[cluster], axis=1)
    returned_best = lax.all_to_all(
        best.reshape(owners, capacity), "blk", split_axis=0, concat_axis=0, tiled=True
    )
    nearest = returned_best.reshape(slots)[position]
    return (nearest, centroid_cosine)


def solution(mesh):
    return jax.shard_map(
        body,
        mesh=mesh,
        in_specs=(
            P(("groups", "blk", "span"), None),
            P(("groups", "blk", "span"), None),
            P(("groups", "blk", "span")),
            P("groups"),
        ),
        out_specs=(P(("groups", "blk", "span")), P(("groups", "blk", "span"))),
        check_vma=False,
    )
```

profile of v0, /device:TPU:0, one launch (start us, length us, event | category | flops | bytes accessed | tf_op | source)
XLA Modules:
  0.0 191.0 jit_solution(9322189716579336675)
XLA Ops:
  8.0 0.0 copy-start.3
  8.0 1.2 fusion
  9.2 0.7 fusion.10
  9.9 0.6 reduce-window.15
  10.5 0.2 slice_reduce_fusion
  10.8 0.8 fusion.9
  11.5 0.7 compare_select_fusion.2
  12.2 3.1 %scatter_custom_fusion.1 = bf16[512,768]{1,0:T(8,128)(2,1)} fusion(s32[256]{0:T(256)S(1)} %bitcast.54, bf16[]{:T(256)} %constant.23.clone.1, bf16[256,768]{1,0:T(8,128)(2,1)} %param.4, f32[256]{0:T(256)S(1)} %add_rsqrt_fusion), kind=kCustom, calls=%fused_computation.18 | custom fusion | flops 589824 | bytes 1180674 | tf_op jit(solution)/shard_map/scatter | solution.py:48
  15.3 7.3 %all-to-all-start.1 = ((bf16[8,64,768]{2,1,0:T(8,128)(2,1)}), bf16[8,64,768]{2,1,0:T(8,128)(2,1)S(1)}, u32[]{:S(2)}, u32[]{:S(2)}) async-start(bf16[8,64,768]{2,1,0:T(8,128)(2,1)} %bitcast.7), calls=%async_computation.1 | async-start | bytes 1572864 | tf_op jit(solution)/shard_map/all_to_all | solution.py:51
  22.6 0.0 all-reduce.2.cloned.1.call-start
  22.7 0.2 select_reduce_fusion.5
  22.9 1.1 fusion.6
  24.0 0.0 all-reduce.2.cloned.1.call-update
  24.1 1.4 scatter_custom_fusion
  25.5 0.7 all_to_all.13
  26.1 0.6 iota_add_fusion
  26.7 16.9 %all-to-all-done.1 = bf16[8,64,768]{2,1,0:T(8,128)(2,1)S(1)} async-done(((bf16[8,64,768]{2,1,0:T(8,128)(2,1)}), bf16[8,64,768]{2,1,0:T(8,128)(2,1)S(1)}, u32[]{:S(2)}, u32[]{:S(2)}) %all-to-all-start.1) | async-done | bytes 786464 | tf_op jit(solution)/shard_map/all_to_all | solution.py:51
  43.6 3.5 %all-to-all-start = ((s32[8,1,64]{2,1,0:T(1,128)}), s32[8,1,64]{2,1,0:T(1,128)S(1)}, u32[]{:S(2)}, u32[]{:S(2)}) async-start(s32[8,1,64]{2,1,0:T(1,128)} %all_to_all.13), calls=%async_computation | async-start | bytes 8192 | tf_op jit(solution)/shard_map/all_to_all | solution.py:58
  47.1 0.0 all-gather.3.cloned.1.call-start
  47.1 0.5 all-gather.3.cloned.1.call-update
  47.7 0.6 pad_clamp_fusion
  48.3 0.1 dynamic-slice_add_fusion
  48.3 5.2 %all-to-all-done = s32[8,1,64]{2,1,0:T(1,128)S(1)} async-done(((s32[8,1,64]{2,1,0:T(1,128)}), s32[8,1,64]{2,1,0:T(1,128)S(1)}, u32[]{:S(2)}, u32[]{:S(2)}) %all-to-all-start) | async-done | bytes 2080 | tf_op jit(solution)/shard_map/all_to_all | solution.py:58
  53.6 0.1 reshape.217
  53.7 1.8 all-gather
  55.5 0.3 reduce-window.19
  55.8 0.1 slice.19
  55.9 0.1 slice_reduce_fusion.1
  56.0 0.1 compare_select_fusion
  56.1 4.3 %scatter_custom_fusion.2 = s32[256]{0:T(256)S(1)} fusion(s32[1024]{0:T(1024)S(1)} %compare_select_fusion, s32[1024]{0:T(1024)S(1)} %bitcast.49, s32[]{:T(128)} %constant.19.clone.1), kind=kCustom, calls=%fused_computation.53 | custom fusion | bytes 1028 | tf_op jit(solution)/shard_map/scatter | solution.py:82
  60.4 1.3 collective-permute-start.2
  61.7 5.1 %collective-permute-start = (s32[256]{0:T(256)S(1)}, s32[256]{0:T(256)}, u32[]{:S(2)}, u32[]{:S(2)}) collective-permute-start(s32[256]{0:T(256)S(1)} %scatter_custom_fusion.2), channel_id=1, source_target_pairs={{0,2},{2,4},{4,6},{6,8},{8,10},{10,12},{12,14},{1,3},{3,5},{5,7},{... | collective-permute-start | bytes 3080 | tf_op jit(solution)/shard_map/ppermute | solution.py:12
  66.8 0.5 broadcast.121
  67.3 0.7 reduce.12
  68.0 0.1 eq.145
  68.1 0.5 broadcast_compare_fusion.1
  68.6 1.3 collective-permute-start.6
  69.9 5.1 %collective-permute-start.4 = (s32[256]{0:T(256)}, s32[256]{0:T(256)}, u32[]{:S(2)}, u32[]{:S(2)}) collective-permute-start(s32[256]{0:T(256)} %collective-permute-done), channel_id=1, source_target_pairs={{0,2},{2,4},{4,6},{6,8},{8,10},{10,12},{12,14},{1,3},{3,5},{5,7},{... | collective-permute-start | bytes 3080 | tf_op jit(solution)/shard_map/ppermute | solution.py:12
  75.0 47.2 %all-reduce.2.cloned.1.call-done = f32[128,768]{1,0:T(8,128)} async-done(((f32[128,768]{1,0:T(8,128)}), f32[128,768]{1,0:T(8,128)}) %all-reduce.2.cloned.1.call-update) | async-done | bytes 393232 | tf_op jit(solution)/shard_map/psum | solution.py:99
  122.2 1.1 multiply_reduce_fusion.1
  123.4 0.0 all-gather.3.cloned.1.call-done
  123.4 5.7 %scatter_custom_fusion.3 = bf16[256,768]{1,0:T(8,128)(2,1)S(1)} fusion(s32[1024]{0:T(1024)S(1)} %compare_select_fusion, bf16[1024,768]{1,0:T(8,128)(2,1)} %all-gather.3.cloned.1.call-done, bf16[]{:T(256)} %constant.23.clone.1), kind=kCustom, calls=%fused_computation.21 | custom fusion | bytes 393728 | tf_op jit(solution)/shard_map/scatter | solution.py:81
  129.1 1.3 collective-permute-start.3
  130.4 4.6 %collective-permute-start.1 = (bf16[256,768]{1,0:T(8,128)(2,1)S(1)}, bf16[256,768]{1,0:T(8,128)(2,1)S(1)}, u32[]{:S(2)}, u32[]{:S(2)}) collective-permute-start(bf16[256,768]{1,0:T(8,128)(2,1)S(1)} %scatter_custom_fusion.3), channel_id=1, source_target_pairs={{0,2},{2,4},{4,6},{6,8},{8,10},{10,12},{12,14},{1,3},{3,5},{5,7},{... | collective-permute-start | bytes 1179656 | tf_op jit(solution)/shard_map/ppermute | solution.py:12
  135.0 1.1 broadcast_divide_fusion
  136.1 1.4 gather_fusion.1
  137.5 2.8 %select_reduce_fusion = f32[512]{0:T(512)S(1)} fusion(bf16[512,768]{1,0:T(8,128)(2,1)S(1)} %bitcast.41, bf16[1024,768]{1,0:T(8,128)(2,1)} %all-gather.3.cloned.1.call-done, s32[1024]{0:T(1024)S(1)} %bitcast.50, s32[512]{0:T(512)} %iota_add_fusion, s32[512]{0:T(512)S(1)} %eq.145, pred[512]{0:T(512)(128)(4,1)} %broadcast_compare_fusion.1), kind=kOutput, calls=%fused_computation.6 | convolution fusion | flops 808451584 | bytes 2370048 | tf_op jit(solution)/shard_map/dot_general | solution.py:22
  140.3 0.7 collective-permute-done.3
  141.0 1.3 collective-permute-start.7
  142.3 6.2 %collective-permute-done.1 = bf16[256,768]{1,0:T(8,128)(2,1)S(1)} collective-permute-done((bf16[256,768]{1,0:T(8,128)(2,1)S(1)}, bf16[256,768]{1,0:T(8,128)(2,1)S(1)}, u32[]{:S(2)}, u32[]{:S(2)}) %collective-permute-start.1) | collective-permute-done | bytes 393248 | tf_op jit(solution)/shard_map/ppermute | solution.py:12
  148.5 4.4 %collective-permute-start.5 = (bf16[256,768]{1,0:T(8,128)(2,1)S(1)}, bf16[256,768]{1,0:T(8,128)(2,1)S(1)}, u32[]{:S(2)}, u32[]{:S(2)}) collective-permute-start(bf16[256,768]{1,0:T(8,128)(2,1)S(1)} %collective-permute-done.1), channel_id=1, source_target_pairs={{0,2},{2,4},{4,6},{6,8},{8,10},{10,12},{12,14},{1,3},{3,5},{5,7},{... | collective-permute-start | bytes 1179656 | tf_op jit(solution)/shard_map/ppermute | solution.py:12
  152.9 0.4 fusion.17
  153.3 0.4 fusion.18
  153.7 0.4 fusion.19
  154.1 11.3 %collective-permute-done.5 = bf16[256,768]{1,0:T(8,128)(2,1)S(1)} collective-permute-done((bf16[256,768]{1,0:T(8,128)(2,1)S(1)}, bf16[256,768]{1,0:T(8,128)(2,1)S(1)}, u32[]{:S(2)}, u32[]{:S(2)}) %collective-permute-start.5) | collective-permute-done | bytes 393248 | tf_op jit(solution)/shard_map/ppermute | solution.py:12
  165.4 1.3 select_reduce_fusion.4
  166.7 0.7 max.65
  167.4 5.9 %all-to-all-start.2 = ((f32[8,1,64]{2,1,0:T(1,128)}), f32[8,1,64]{2,1,0:T(1,128)S(1)}, u32[]{:S(2)}, u32[]{:S(2)}) async-start(f32[8,1,64]{2,1,0:T(1,128)} %max.65), calls=%async_computation.2 | async-start | bytes 8192 | tf_op jit(solution)/shard_map/all_to_all | solution.py:103
  173.3 0.8 multiply_reduce_fusion
  174.1 5.7 %all-to-all-done.2 = f32[8,1,64]{2,1,0:T(1,128)S(1)} async-done(((f32[8,1,64]{2,1,0:T(1,128)}), f32[8,1,64]{2,1,0:T(1,128)S(1)}, u32[]{:S(2)}, u32[]{:S(2)}) %all-to-all-start.2) | async-done | bytes 2080 | tf_op jit(solution)/shard_map/all_to_all | solution.py:103
  179.8 0.5 broadcast.122
  180.3 0.7 reduce.13
  181.0 0.1 reshape.165
  181.1 2.5 %gather_fusion = f32[256]{0:T(256)} fusion(f32[512]{0:T(512)S(1)} %reshape.165, s32[1024]{0:T(1024)S(1)} %pad_clamp_fusion.1), kind=kCustom, calls=%fused_computation | custom fusion | bytes 3072 | tf_op jit(solution)/shard_map/gather | solution.py:106
  (29 shorter events, 0.2 us)
Async XLA Ops:
  8.0 14.9 %copy-start.2 = (bf16[256,768]{1,0:T(8,128)(2,1)S(1)}, bf16[256,768]{1,0:T(8,128)(2,1)}, u32[]{:S(2)}) copy-start(bf16[256,768]{1,0:T(8,128)(2,1)} %param.4) | copy-start | bytes 1179652
  8.0 14.7 %copy-start.3 = (s32[256,1]{0,1:T(1,128)S(1)}, s32[256,1]{0,1:T(1,128)}, u32[]{:S(2)}) copy-start(s32[256,1]{0,1:T(1,128)} %param.5) | copy-start | bytes 3076
  8.0 14.7 %copy-start.4 = (s32[256]{0:T(256)S(1)}, s32[256]{0:T(256)}, u32[]{:S(2)}) copy-start(s32[256]{0:T(256)} %param.6) | copy-start | bytes 3076
  8.0 14.7 %copy-start.5 = (s32[128]{0:T(128)S(1)}, s32[128]{0:T(128)}, u32[]{:S(2)}) copy-start(s32[128]{0:T(128)} %param.7) | copy-start | bytes 1540
  15.3 28.3 %all-to-all-start.1 = ((bf16[8,64,768]{2,1,0:T(8,128)(2,1)}), bf16[8,64,768]{2,1,0:T(8,128)(2,1)S(1)}, u32[]{:S(2)}, u32[]{:S(2)}) async-start(bf16[8,64,768]{2,1,0:T(8,128)(2,1)} %bitcast.7), calls=%async_computation.1 | async-start | bytes 1572864 | tf_op jit(solution)/shard_map/all_to_all | solution.py:51
  22.6 99.6 %all-reduce.2.cloned.1.call-start = ((), (), s32[]{:S(2)}) async-start(), calls=%async_computation.4 | async-start | bytes 786432 | tf_op jit(solution)/shard_map/psum | solution.py:99
  43.6 3.5 %copy-start = (bf16[8,64,768]{2,1,0:T(8,128)(2,1)}, bf16[8,64,768]{2,1,0:T(8,128)(2,1)S(1)}, u32[]{:S(2)}) copy-start(bf16[8,64,768]{2,1,0:T(8,128)(2,1)S(1)} %all-to-all-done.1) | copy-start | bytes 2359300
  43.6 10.0 %all-to-all-start = ((s32[8,1,64]{2,1,0:T(1,128)}), s32[8,1,64]{2,1,0:T(1,128)S(1)}, u32[]{:S(2)}, u32[]{:S(2)}) async-start(s32[8,1,64]{2,1,0:T(1,128)} %all_to_all.13), calls=%async_computation | async-start | bytes 8192 | tf_op jit(solution)/shard_map/all_to_all | solution.py:58
  47.1 76.3 %all-gather.3.cloned.1.call-start = ((), (), s32[]{:S(2)}) async-start(), calls=%async_computation.3 | async-start | bytes 2359296 | tf_op jit(solution)/shard_map/all_gather | solution.py:65
  60.4 8.2 %collective-permute-start.2 = (s32[256]{0:T(256)S(1)}, s32[256]{0:T(256)}, u32[]{:S(2)}, u32[]{:S(2)}) collective-permute-start(s32[256]{0:T(256)S(1)} %scatter_custom_fusion.2), channel_id=1, source_target_pairs={{2,0},{4,2},{6,4},{8,6},{10,8},{12,10},{14,12},{3,1},{5,3},{7,5},{... | collective-permute-start | bytes 3080 | tf_op jit(solution)/shard_map/ppermute | solution.py:12
  61.7 8.2 %collective-permute-start = (s32[256]{0:T(256)S(1)}, s32[256]{0:T(256)}, u32[]{:S(2)}, u32[]{:S(2)}) collective-permute-start(s32[256]{0:T(256)S(1)} %scatter_custom_fusion.2), channel_id=1, source_target_pairs={{0,2},{2,4},{4,6},{6,8},{8,10},{10,12},{12,14},{1,3},{3,5},{5,7},{... | collective-permute-start | bytes 3080 | tf_op jit(solution)/shard_map/ppermute | solution.py:12
  68.6 85.5 %collective-permute-start.6 = (s32[256]{0:T(256)}, s32[256]{0:T(256)}, u32[]{:S(2)}, u32[]{:S(2)}) collective-permute-start(s32[256]{0:T(256)} %collective-permute-done.2), channel_id=1, source_target_pairs={{2,0},{4,2},{6,4},{8,6},{10,8},{12,10},{14,12},{3,1},{5,3},{7,5},{... | collective-permute-start | bytes 3080 | tf_op jit(solution)/shard_map/ppermute | solution.py:12
  69.9 84.3 %collective-permute-start.4 = (s32[256]{0:T(256)}, s32[256]{0:T(256)}, u32[]{:S(2)}, u32[]{:S(2)}) collective-permute-start(s32[256]{0:T(256)} %collective-permute-done), channel_id=1, source_target_pairs={{0,2},{2,4},{4,6},{6,8},{8,10},{10,12},{12,14},{1,3},{3,5},{5,7},{... | collective-permute-start | bytes 3080 | tf_op jit(solution)/shard_map/ppermute | solution.py:12
  129.1 11.9 %collective-permute-start.3 = (bf16[256,768]{1,0:T(8,128)(2,1)S(1)}, bf16[256,768]{1,0:T(8,128)(2,1)S(1)}, u32[]{:S(2)}, u32[]{:S(2)}) collective-permute-start(bf16[256,768]{1,0:T(8,128)(2,1)S(1)} %scatter_custom_fusion.3), channel_id=1, source_target_pairs={{2,0},{4,2},{6,4},{8,6},{10,8},{12,10},{14,12},{3,1},{5,3},{7,5},{... | collective-permute-start | bytes 1179656 | tf_op jit(solution)/shard_map/ppermute | solution.py:12
  130.4 18.0 %collective-permute-start.1 = (bf16[256,768]{1,0:T(8,128)(2,1)S(1)}, bf16[256,768]{1,0:T(8,128)(2,1)S(1)}, u32[]{:S(2)}, u32[]{:S(2)}) collective-permute-start(bf16[256,768]{1,0:T(8,128)(2,1)S(1)} %scatter_custom_fusion.3), channel_id=1, source_target_pairs={{0,2},{2,4},{4,6},{6,8},{8,10},{10,12},{12,14},{1,3},{3,5},{5,7},{... | collective-permute-start | bytes 1179656 | tf_op jit(solution)/shard_map/ppermute | solution.py:12
  136.1 1.4 copy-start.1
  141.0 12.7 %collective-permute-start.7 = (bf16[256,768]{1,0:T(8,128)(2,1)S(1)}, bf16[256,768]{1,0:T(8,128)(2,1)S(1)}, u32[]{:S(2)}, u32[]{:S(2)}) collective-permute-start(bf16[256,768]{1,0:T(8,128)(2,1)S(1)} %collective-permute-done.3), channel_id=1, source_target_pairs={{2,0},{4,2},{6,4},{8,6},{10,8},{12,10},{14,12},{3,1},{5,3},{7,5},{... | collective-permute-start | bytes 1179656 | tf_op jit(solution)/shard_map/ppermute | solution.py:12
  148.5 17.0 %collective-permute-start.5 = (bf16[256,768]{1,0:T(8,128)(2,1)S(1)}, bf16[256,768]{1,0:T(8,128)(2,1)S(1)}, u32[]{:S(2)}, u32[]{:S(2)}) collective-permute-start(bf16[256,768]{1,0:T(8,128)(2,1)S(1)} %collective-permute-done.1), channel_id=1, source_target_pairs={{0,2},{2,4},{4,6},{6,8},{8,10},{10,12},{12,14},{1,3},{3,5},{5,7},{... | collective-permute-start | bytes 1179656 | tf_op jit(solution)/shard_map/ppermute | solution.py:12
  153.3 12.2 %copy-start.6 = (pred[512]{0:T(512)(128)(4,1)S(1)}, pred[512]{0:T(512)(128)(4,1)}, u32[]{:S(2)}) copy-start(pred[512]{0:T(512)(128)(4,1)} %broadcast_compare_fusion.1) | copy-start | bytes 1540
  167.4 12.4 %all-to-all-start.2 = ((f32[8,1,64]{2,1,0:T(1,128)}), f32[8,1,64]{2,1,0:T(1,128)S(1)}, u32[]{:S(2)}, u32[]{:S(2)}) async-start(f32[8,1,64]{2,1,0:T(1,128)} %max.65), calls=%async_computation.2 | async-start | bytes 8192 | tf_op jit(solution)/shard_map/all_to_all | solution.py:103
Sparse Core Ops, SparseCore 0:
  26.8 95.4 all-reduce.1
Sparse Core Ops, SparseCore 1:
  49.1 11.1 all-gather.2
where the time goes:
time: 192 us; the launch traced here: 191 us
  waiting for transfers between devices  93.8 us (49%)
  starting transfers between devices  41.1 us (21%)
  local copies, waits for them, and re-layouts  18.3 us (10%)
  between operations  15.8 us (8%)
  other arithmetic  13.8 us (7%)
  matrix products  6.34 us (3%)
    psum x1, waiting for transfers between devices, body(): sums = lax.psum(partial_sums, ('blk', 'span'))  47.2 us
    ppermute x8, starting transfers between devices, passed_along(): lax.ppermute(value, axis, [(source, source + steps) for source in range(f...  24.3 us
    ppermute x8, waiting for transfers between devices, passed_along(): lax.ppermute(value, axis, [(source, source + steps) for source in range(f...  18.2 us
    all_to_all x1, waiting for transfers between devices, body(): lax.all_to_all(send_rows.reshape(owners, capacity, width), 'blk', split_a...  16.9 us
    all_to_all x1, starting transfers between devices, body(): lax.all_to_all(send_rows.reshape(owners, capacity, width), 'blk', split_a...  7.31 us
    all_to_all x1, starting transfers between devices, body(): lax.all_to_all(best.reshape(owners, capacity), 'blk', split_axis=0, conca...  5.92 us
    scatter x1, local copies, waits for them, and re-layouts, body(): jnp.zeros((share_limit, width), jnp.bfloat16).at[target]  5.74 us
    all_to_all x1, waiting for transfers between devices, body(): lax.all_to_all(best.reshape(owners, capacity), 'blk', split_axis=0, conca...  5.68 us
  transfers between devices with their start and end apart: 13, of which 7 were waited for; matrix products, arithmetic and copies ran while one was open for 13% of the time, Pallas kernels for 0%

commit v1 on v0

--- a/solution.py
+++ b/solution.py
@@ -96,7 +96,7 @@
         (((0,), (0,)), ((), ())),
         preferred_element_type=jnp.float32,
     )
-    sums = lax.psum(partial_sums, ("blk", "span"))
+    sums = lax.psum(lax.psum(partial_sums, "span"), "blk")
     length = jnp.sqrt(jnp.sum(sums * sums, axis=1, keepdims=True))
     direction = sums / jnp.maximum(length, 1.0)
     centroid_cosine = jnp.sum(unit.astype(jnp.float32) * direction[cluster], axis=1)

time: 192 us -> 205 us (1.068)
  waiting for transfers between devices: 93.8 us -> 106 us
  starting transfers between devices: 41.1 us -> 43.9 us
    all_to_all x1, waiting for transfers between devices: 16.9 us -> 0.01 us  [body(): lax.all_to_all(send_rows.reshape(owners, capacity, width), 'blk', split_a...]
    psum x1 -> x2, waiting for transfers between devices: 47.2 us -> 61.4 us  [body(): sums = lax.psum(lax.psum(partial_sums, 'span'), 'blk')]
    all_gather x1, waiting for transfers between devices: 0.03 us -> 9.31 us  [body(): lax.all_gather(mine, 'span', axis=0, tiled=True)]
    ppermute x8, waiting for transfers between devices: 18.2 us -> 23.3 us  [passed_along(): lax.ppermute(value, axis, [(source, source + steps) for source in range(f...]
    all_to_all x1, starting transfers between devices: 3.48 us -> 5.83 us  [body(): lax.all_to_all(send_tags.reshape(owners, capacity), 'blk', split_axis=0,...]
  transfers between devices with their start and end apart: 13 -> 14, of which waited for: 7 -> 8; matrix products, arithmetic and copies ran while one was open for 13% -> 12% of each run, Pallas kernels for 0% -> 0%
where the time goes in v1:
time: 205 us; the launch traced here: 204 us
  waiting for transfers between devices  106 us (52%)
  starting transfers between devices  43.9 us (21%)
  local copies, waits for them, and re-layouts  18.3 us (9%)
  between operations  14.1 us (7%)
  other arithmetic  13.8 us (7%)
  matrix products  6.31 us (3%)
    psum x2, waiting for transfers between devices, body(): sums = lax.psum(lax.psum(partial_sums, 'span'), 'blk')  61.4 us
    ppermute x8, starting transfers between devices, passed_along(): lax.ppermute(value, axis, [(source, source + steps) for source in range(f...  24.3 us
    ppermute x8, waiting for transfers between devices, passed_along(): lax.ppermute(value, axis, [(source, source + steps) for source in range(f...  23.3 us
    all_gather x1, waiting for transfers between devices, body(): lax.all_gather(mine, 'span', axis=0, tiled=True)  9.31 us
    all_to_all x1, starting transfers between devices, body(): lax.all_to_all(send_rows.reshape(owners, capacity, width), 'blk', split_a...  7.31 us
    all_to_all x1, starting transfers between devices, body(): lax.all_to_all(best.reshape(owners, capacity), 'blk', split_axis=0, conca...  6.32 us
    all_to_all x1, starting transfers between devices, body(): lax.all_to_all(send_tags.reshape(owners, capacity), 'blk', split_axis=0,...  5.83 us
    scatter x1, local copies, waits for them, and re-layouts, body(): jnp.zeros((share_limit, width), jnp.bfloat16).at[target]  5.73 us
  transfers between devices with their start and end apart: 14, of which 8 were waited for; matrix products, arithmetic and copies ran while one was open for 12% of the time, Pallas kernels for 0%

profile of v1, /device:TPU:0, one launch (start us, length us, event | category | flops | bytes accessed | tf_op | source)
XLA Modules:
  0.0 203.8 jit_solution(13111134576609811754)
XLA Ops:
  7.2 1.2 fusion
  8.4 0.7 fusion.10
  9.1 0.6 reduce-window.15
  9.7 0.2 slice_reduce_fusion
  9.9 0.8 fusion.9
  10.7 0.7 compare_select_fusion.2
  11.4 3.1 %scatter_custom_fusion.1 = bf16[512,768]{1,0:T(8,128)(2,1)} fusion(s32[256]{0:T(256)S(1)} %bitcast.54, bf16[]{:T(256)} %constant.23.clone.1, bf16[256,768]{1,0:T(8,128)(2,1)} %param.4, f32[256]{0:T(256)S(1)} %add_rsqrt_fusion), kind=kCustom, calls=%fused_computation.18 | custom fusion | flops 589824 | bytes 1180674 | tf_op jit(solution)/shard_map/scatter | solution.py:48
  14.5 7.3 %all-to-all-start.1 = ((bf16[8,64,768]{2,1,0:T(8,128)(2,1)}), bf16[8,64,768]{2,1,0:T(8,128)(2,1)S(1)}, u32[]{:S(2)}, u32[]{:S(2)}) async-start(bf16[8,64,768]{2,1,0:T(8,128)(2,1)} %bitcast.7), calls=%async_computation.1 | async-start | bytes 1572864 | tf_op jit(solution)/shard_map/all_to_all | solution.py:51
  21.8 0.0 all-reduce.3.cloned.1.call-start
  21.9 0.2 select_reduce_fusion.5
  22.1 1.1 fusion.6
  23.2 0.0 all-reduce.5.cloned.1.call-start
  23.2 21.5 %all-reduce.3.cloned.1.call-done = f32[128,768]{1,0:T(8,128)} async-done(((f32[128,768]{1,0:T(8,128)}), f32[128,768]{1,0:T(8,128)}) %all-reduce.3.cloned.1.call-update) | async-done | bytes 393232 | tf_op jit(solution)/shard_map/psum | solution.py:99
  44.8 0.0 all-reduce.5.cloned.1.call-update
  44.8 1.4 scatter_custom_fusion
  46.2 0.7 all_to_all.13
  46.9 0.6 iota_add_fusion
  47.5 5.8 %all-to-all-start = ((s32[8,1,64]{2,1,0:T(1,128)}), s32[8,1,64]{2,1,0:T(1,128)S(1)}, u32[]{:S(2)}, u32[]{:S(2)}) async-start(s32[8,1,64]{2,1,0:T(1,128)} %all_to_all.13), calls=%async_computation | async-start | bytes 8192 | tf_op jit(solution)/shard_map/all_to_all | solution.py:58
  53.3 0.0 all-gather.3.cloned.1.call-start
  53.4 0.7 all-gather.3.cloned.1.call-update
  54.1 0.6 pad_clamp_fusion
  54.7 0.1 dynamic-slice_add_fusion
  54.8 5.1 %all-to-all-done = s32[8,1,64]{2,1,0:T(1,128)S(1)} async-done(((s32[8,1,64]{2,1,0:T(1,128)}), s32[8,1,64]{2,1,0:T(1,128)S(1)}, u32[]{:S(2)}, u32[]{:S(2)}) %all-to-all-start) | async-done | bytes 2080 | tf_op jit(solution)/shard_map/all_to_all | solution.py:58
  59.8 0.1 reshape.217
  59.9 1.8 all-gather
  61.8 0.3 reduce-window.19
  62.1 0.1 slice.19
  62.2 0.1 slice_reduce_fusion.1
  62.3 0.1 compare_select_fusion
  62.4 4.3 %scatter_custom_fusion.2 = s32[256]{0:T(256)S(1)} fusion(s32[1024]{0:T(1024)S(1)} %compare_select_fusion, s32[1024]{0:T(1024)S(1)} %bitcast.49, s32[]{:T(128)} %constant.19.clone.1), kind=kCustom, calls=%fused_computation.53 | custom fusion | bytes 1028 | tf_op jit(solution)/shard_map/scatter | solution.py:82
  66.7 1.3 collective-permute-start.2
  68.0 5.1 %collective-permute-start = (s32[256]{0:T(256)S(1)}, s32[256]{0:T(256)}, u32[]{:S(2)}, u32[]{:S(2)}) collective-permute-start(s32[256]{0:T(256)S(1)} %scatter_custom_fusion.2), channel_id=1, source_target_pairs={{0,2},{2,4},{4,6},{6,8},{8,10},{10,12},{12,14},{1,3},{3,5},{5,7},{... | collective-permute-start | bytes 3080 | tf_op jit(solution)/shard_map/ppermute | solution.py:12
  73.1 0.5 broadcast.121
  73.6 0.7 reduce.12
  74.2 0.1 eq.145
  74.3 0.5 broadcast_compare_fusion.1
  74.8 1.3 collective-permute-start.6
  76.1 5.1 %collective-permute-start.4 = (s32[256]{0:T(256)}, s32[256]{0:T(256)}, u32[]{:S(2)}, u32[]{:S(2)}) collective-permute-start(s32[256]{0:T(256)} %collective-permute-done), channel_id=1, source_target_pairs={{0,2},{2,4},{4,6},{6,8},{8,10},{10,12},{12,14},{1,3},{3,5},{5,7},{... | collective-permute-start | bytes 3080 | tf_op jit(solution)/shard_map/ppermute | solution.py:12
  81.3 39.9 %all-reduce.5.cloned.1.call-done = f32[128,768]{1,0:T(8,128)} async-done(((f32[128,768]{1,0:T(8,128)}), f32[128,768]{1,0:T(8,128)}) %all-reduce.5.cloned.1.call-update) | async-done | bytes 393232 | tf_op jit(solution)/shard_map/psum | solution.py:99
  121.2 1.1 multiply_reduce_fusion.1
  122.3 9.3 %all-gather.3.cloned.1.call-done = bf16[1024,768]{1,0:T(8,128)(2,1)} async-done(((bf16[512,768]{1,0:T(8,128)(2,1)}), bf16[1024,768]{1,0:T(8,128)(2,1)}) %all-gather.3.cloned.1.call-update) | async-done | bytes 1572880 | tf_op jit(solution)/shard_map/all_gather | solution.py:65
  131.6 5.7 %scatter_custom_fusion.3 = bf16[256,768]{1,0:T(8,128)(2,1)S(1)} fusion(s32[1024]{0:T(1024)S(1)} %compare_select_fusion, bf16[1024,768]{1,0:T(8,128)(2,1)} %all-gather.3.cloned.1.call-done, bf16[]{:T(256)} %constant.23.clone.1), kind=kCustom, calls=%fused_computation.21 | custom fusion | bytes 393728 | tf_op jit(solution)/shard_map/scatter | solution.py:81
  137.3 1.3 collective-permute-start.3
  138.6 4.6 %collective-permute-start.1 = (bf16[256,768]{1,0:T(8,128)(2,1)S(1)}, bf16[256,768]{1,0:T(8,128)(2,1)S(1)}, u32[]{:S(2)}, u32[]{:S(2)}) collective-permute-start(bf16[256,768]{1,0:T(8,128)(2,1)S(1)} %scatter_custom_fusion.3), channel_id=1, source_target_pairs={{0,2},{2,4},{4,6},{6,8},{8,10},{10,12},{12,14},{1,3},{3,5},{5,7},{... | collective-permute-start | bytes 1179656 | tf_op jit(solution)/shard_map/ppermute | solution.py:12
  143.2 1.1 broadcast_divide_fusion
  144.3 1.4 gather_fusion.1
  145.7 2.8 %select_reduce_fusion = f32[512]{0:T(512)S(1)} fusion(bf16[512,768]{1,0:T(8,128)(2,1)S(1)} %bitcast.41, bf16[1024,768]{1,0:T(8,128)(2,1)} %all-gather.3.cloned.1.call-done, s32[1024]{0:T(1024)S(1)} %bitcast.50, s32[512]{0:T(512)} %iota_add_fusion, s32[512]{0:T(512)S(1)} %eq.145, pred[512]{0:T(512)(128)(4,1)} %broadcast_compare_fusion.1), kind=kOutput, calls=%fused_computation.6 | convolution fusion | flops 808451584 | bytes 2370048 | tf_op jit(solution)/shard_map/dot_general | solution.py:22
  148.5 2.1 %collective-permute-done.3 = bf16[256,768]{1,0:T(8,128)(2,1)S(1)} collective-permute-done((bf16[256,768]{1,0:T(8,128)(2,1)S(1)}, bf16[256,768]{1,0:T(8,128)(2,1)S(1)}, u32[]{:S(2)}, u32[]{:S(2)}) %collective-permute-start.3) | collective-permute-done | bytes 393248 | tf_op jit(solution)/shard_map/ppermute | solution.py:12
  150.5 1.3 collective-permute-start.7
  151.8 7.3 %collective-permute-done.1 = bf16[256,768]{1,0:T(8,128)(2,1)S(1)} collective-permute-done((bf16[256,768]{1,0:T(8,128)(2,1)S(1)}, bf16[256,768]{1,0:T(8,128)(2,1)S(1)}, u32[]{:S(2)}, u32[]{:S(2)}) %collective-permute-start.1) | collective-permute-done | bytes 393248 | tf_op jit(solution)/shard_map/ppermute | solution.py:12
  159.1 4.4 %collective-permute-start.5 = (bf16[256,768]{1,0:T(8,128)(2,1)S(1)}, bf16[256,768]{1,0:T(8,128)(2,1)S(1)}, u32[]{:S(2)}, u32[]{:S(2)}) collective-permute-start(bf16[256,768]{1,0:T(8,128)(2,1)S(1)} %collective-permute-done.1), channel_id=1, source_target_pairs={{0,2},{2,4},{4,6},{6,8},{8,10},{10,12},{12,14},{1,3},{3,5},{5,7},{... | collective-permute-start | bytes 1179656 | tf_op jit(solution)/shard_map/ppermute | solution.py:12
  163.5 0.4 fusion.17
  163.9 0.4 fusion.18
  164.4 0.4 fusion.19
  164.8 13.9 %collective-permute-done.5 = bf16[256,768]{1,0:T(8,128)(2,1)S(1)} collective-permute-done((bf16[256,768]{1,0:T(8,128)(2,1)S(1)}, bf16[256,768]{1,0:T(8,128)(2,1)S(1)}, u32[]{:S(2)}, u32[]{:S(2)}) %collective-permute-start.5) | collective-permute-done | bytes 393248 | tf_op jit(solution)/shard_map/ppermute | solution.py:12
  178.7 1.3 select_reduce_fusion.4
  180.0 0.7 max.65
  180.7 6.3 %all-to-all-start.2 = ((f32[8,1,64]{2,1,0:T(1,128)}), f32[8,1,64]{2,1,0:T(1,128)S(1)}, u32[]{:S(2)}, u32[]{:S(2)}) async-start(f32[8,1,64]{2,1,0:T(1,128)} %max.65), calls=%async_computation.2 | async-start | bytes 8192 | tf_op jit(solution)/shard_map/all_to_all | solution.py:103
  187.0 0.8 multiply_reduce_fusion
  187.8 5.7 %all-to-all-done.2 = f32[8,1,64]{2,1,0:T(1,128)S(1)} async-done(((f32[8,1,64]{2,1,0:T(1,128)}), f32[8,1,64]{2,1,0:T(1,128)S(1)}, u32[]{:S(2)}, u32[]{:S(2)}) %all-to-all-start.2) | async-done | bytes 2080 | tf_op jit(solution)/shard_map/all_to_all | solution.py:103
  193.5 0.5 broadcast.122
  194.0 0.7 reduce.13
  194.7 0.1 reshape.165
  194.8 2.5 %gather_fusion = f32[256]{0:T(256)} fusion(f32[512]{0:T(512)S(1)} %reshape.165, s32[1024]{0:T(1024)S(1)} %pad_clamp_fusion.1), kind=kCustom, calls=%fused_computation | custom fusion | bytes 3072 | tf_op jit(solution)/shard_map/gather | solution.py:106
  (32 shorter events, 0.2 us)
Async XLA Ops:
  7.2 14.9 %copy-start.2 = (bf16[256,768]{1,0:T(8,128)(2,1)S(1)}, bf16[256,768]{1,0:T(8,128)(2,1)}, u32[]{:S(2)}) copy-start(bf16[256,768]{1,0:T(8,128)(2,1)} %param.4) | copy-start | bytes 1179652
  7.2 14.7 %copy-start.3 = (s32[256,1]{0,1:T(1,128)S(1)}, s32[256,1]{0,1:T(1,128)}, u32[]{:S(2)}) copy-start(s32[256,1]{0,1:T(1,128)} %param.5) | copy-start | bytes 3076
  7.2 14.7 %copy-start.4 = (s32[256]{0:T(256)S(1)}, s32[256]{0:T(256)}, u32[]{:S(2)}) copy-start(s32[256]{0:T(256)} %param.6) | copy-start | bytes 3076
  7.2 14.7 %copy-start.5 = (s32[128]{0:T(128)S(1)}, s32[128]{0:T(128)}, u32[]{:S(2)}) copy-start(s32[128]{0:T(128)} %param.7) | copy-start | bytes 1540
  14.5 33.0 %all-to-all-start.1 = ((bf16[8,64,768]{2,1,0:T(8,128)(2,1)}), bf16[8,64,768]{2,1,0:T(8,128)(2,1)S(1)}, u32[]{:S(2)}, u32[]{:S(2)}) async-start(bf16[8,64,768]{2,1,0:T(8,128)(2,1)} %bitcast.7), calls=%async_computation.1 | async-start | bytes 1572864 | tf_op jit(solution)/shard_map/all_to_all | solution.py:51
  21.8 23.0 %all-reduce.3.cloned.1.call-start = ((), (), s32[]{:S(2)}) async-start(), calls=%async_computation.4 | async-start | bytes 786432 | tf_op jit(solution)/shard_map/psum | solution.py:99
  23.2 98.0 %all-reduce.5.cloned.1.call-start = ((), (), s32[]{:S(2)}) async-start(), calls=%async_computation.5 | async-start | bytes 786432 | tf_op jit(solution)/shard_map/psum | solution.py:99
  47.5 5.9 %copy-start = (bf16[8,64,768]{2,1,0:T(8,128)(2,1)}, bf16[8,64,768]{2,1,0:T(8,128)(2,1)S(1)}, u32[]{:S(2)}) copy-start(bf16[8,64,768]{2,1,0:T(8,128)(2,1)S(1)} %all-to-all-done.1) | copy-start | bytes 2359300
  47.5 12.3 %all-to-all-start = ((s32[8,1,64]{2,1,0:T(1,128)}), s32[8,1,64]{2,1,0:T(1,128)S(1)}, u32[]{:S(2)}, u32[]{:S(2)}) async-start(s32[8,1,64]{2,1,0:T(1,128)} %all_to_all.13), calls=%async_computation | async-start | bytes 8192 | tf_op jit(solution)/shard_map/all_to_all | solution.py:58
  53.3 78.3 %all-gather.3.cloned.1.call-start = ((), (), s32[]{:S(2)}) async-start(), calls=%async_computation.3 | async-start | bytes 2359296 | tf_op jit(solution)/shard_map/all_gather | solution.py:65
  66.7 8.2 %collective-permute-start.2 = (s32[256]{0:T(256)S(1)}, s32[256]{0:T(256)}, u32[]{:S(2)}, u32[]{:S(2)}) collective-permute-start(s32[256]{0:T(256)S(1)} %scatter_custom_fusion.2), channel_id=1, source_target_pairs={{2,0},{4,2},{6,4},{8,6},{10,8},{12,10},{14,12},{3,1},{5,3},{7,5},{... | collective-permute-start | bytes 3080 | tf_op jit(solution)/shard_map/ppermute | solution.py:12
  68.0 8.2 %collective-permute-start = (s32[256]{0:T(256)S(1)}, s32[256]{0:T(256)}, u32[]{:S(2)}, u32[]{:S(2)}) collective-permute-start(s32[256]{0:T(256)S(1)} %scatter_custom_fusion.2), channel_id=1, source_target_pairs={{0,2},{2,4},{4,6},{6,8},{8,10},{10,12},{12,14},{1,3},{3,5},{5,7},{... | collective-permute-start | bytes 3080 | tf_op jit(solution)/shard_map/ppermute | solution.py:12
  74.8 89.9 %collective-permute-start.6 = (s32[256]{0:T(256)}, s32[256]{0:T(256)}, u32[]{:S(2)}, u32[]{:S(2)}) collective-permute-start(s32[256]{0:T(256)} %collective-permute-done.2), channel_id=1, source_target_pairs={{2,0},{4,2},{6,4},{8,6},{10,8},{12,10},{14,12},{3,1},{5,3},{7,5},{... | collective-permute-start | bytes 3080 | tf_op jit(solution)/shard_map/ppermute | solution.py:12
  76.1 88.6 %collective-permute-start.4 = (s32[256]{0:T(256)}, s32[256]{0:T(256)}, u32[]{:S(2)}, u32[]{:S(2)}) collective-permute-start(s32[256]{0:T(256)} %collective-permute-done), channel_id=1, source_target_pairs={{0,2},{2,4},{4,6},{6,8},{8,10},{10,12},{12,14},{1,3},{3,5},{5,7},{... | collective-permute-start | bytes 3080 | tf_op jit(solution)/shard_map/ppermute | solution.py:12
  137.3 13.2 %collective-permute-start.3 = (bf16[256,768]{1,0:T(8,128)(2,1)S(1)}, bf16[256,768]{1,0:T(8,128)(2,1)S(1)}, u32[]{:S(2)}, u32[]{:S(2)}) collective-permute-start(bf16[256,768]{1,0:T(8,128)(2,1)S(1)} %scatter_custom_fusion.3), channel_id=1, source_target_pairs={{2,0},{4,2},{6,4},{8,6},{10,8},{12,10},{14,12},{3,1},{5,3},{7,5},{... | collective-permute-start | bytes 1179656 | tf_op jit(solution)/shard_map/ppermute | solution.py:12
  138.6 20.5 %collective-permute-start.1 = (bf16[256,768]{1,0:T(8,128)(2,1)S(1)}, bf16[256,768]{1,0:T(8,128)(2,1)S(1)}, u32[]{:S(2)}, u32[]{:S(2)}) collective-permute-start(bf16[256,768]{1,0:T(8,128)(2,1)S(1)} %scatter_custom_fusion.3), channel_id=1, source_target_pairs={{0,2},{2,4},{4,6},{6,8},{8,10},{10,12},{12,14},{1,3},{3,5},{5,7},{... | collective-permute-start | bytes 1179656 | tf_op jit(solution)/shard_map/ppermute | solution.py:12
  144.3 1.4 copy-start.1
  150.5 13.8 %collective-permute-start.7 = (bf16[256,768]{1,0:T(8,128)(2,1)S(1)}, bf16[256,768]{1,0:T(8,128)(2,1)S(1)}, u32[]{:S(2)}, u32[]{:S(2)}) collective-permute-start(bf16[256,768]{1,0:T(8,128)(2,1)S(1)} %collective-permute-done.3), channel_id=1, source_target_pairs={{2,0},{4,2},{6,4},{8,6},{10,8},{12,10},{14,12},{3,1},{5,3},{7,5},{... | collective-permute-start | bytes 1179656 | tf_op jit(solution)/shard_map/ppermute | solution.py:12
  159.1 19.6 %collective-permute-start.5 = (bf16[256,768]{1,0:T(8,128)(2,1)S(1)}, bf16[256,768]{1,0:T(8,128)(2,1)S(1)}, u32[]{:S(2)}, u32[]{:S(2)}) collective-permute-start(bf16[256,768]{1,0:T(8,128)(2,1)S(1)} %collective-permute-done.1), channel_id=1, source_target_pairs={{0,2},{2,4},{4,6},{6,8},{8,10},{10,12},{12,14},{1,3},{3,5},{5,7},{... | collective-permute-start | bytes 1179656 | tf_op jit(solution)/shard_map/ppermute | solution.py:12
  163.9 14.8 %copy-start.6 = (pred[512]{0:T(512)(128)(4,1)S(1)}, pred[512]{0:T(512)(128)(4,1)}, u32[]{:S(2)}) copy-start(pred[512]{0:T(512)(128)(4,1)} %broadcast_compare_fusion.1) | copy-start | bytes 1540
  180.7 12.8 %all-to-all-start.2 = ((f32[8,1,64]{2,1,0:T(1,128)}), f32[8,1,64]{2,1,0:T(1,128)S(1)}, u32[]{:S(2)}, u32[]{:S(2)}) async-start(f32[8,1,64]{2,1,0:T(1,128)} %max.65), calls=%async_computation.2 | async-start | bytes 8192 | tf_op jit(solution)/shard_map/all_to_all | solution.py:103
Sparse Core Ops, SparseCore 0:
  24.9 19.7 all-reduce.2
  48.1 72.9 all-reduce.4
  122.7 8.8 all-gather.2
